TPU v7x, 512 devices: a whole 4x8x8 slice. The times are simulated.
512 devices in a mesh: dp: 64 (over z, y), member: 8 (over x, core).
Axes of the slice: x: 4, y: 8, z: 8, core: 2. Of those that a mesh axis runs over, the one named last changes fastest.
Arguments:
- inputs: bfloat16 [98304, 393], P(('dp', 'member')), may hold values from -256 to 256
- targets: bfloat16 [98304, 377], P(('dp', 'member')), may hold values from -6 to 6
- bootstrap: int32 [8, 98304], P('member', 'dp'), may hold values from 0 to 1535
- lower_weight: bfloat16 [8, 393, 1024], P('member'), may hold values from -0.3125 to 0.3125
- lower_shift: float32 [8, 1024], P('member'), may hold values from -3 to 3
- upper_weight: bfloat16 [8, 1024, 377], P('member'), may hold values from -0.1875 to 0.1875
- upper_shift: float32 [8, 377], P('member'), may hold values from -3 to 3
- log_var: float32 [8, 377], P('member'), may hold values from -1 to 1
Outputs:
- lower_grad: float32 [8, 1024, 393], P('member', 'dp')
- bias_grad: float32 [8, 1024], P('member', 'dp')
- upper_grad: float32 [8, 1024, 377], P('member', 'dp')
- offset_grad: float32 [8, 377], P('member')
- noise_grad: float32 [8, 377], P('member')
- member_loss: float32 [8], P('member')
Inputs may be any that keep to these rules, and one draw needn't show every extreme that they name: bootstrap[m, r] is an offset within the aligned block of 1536 rows that holds row r.
All inputs are finite; a program needn't handle non-finite values.
Results may differ from a plain program's by a relative error of at most 0.00076.
Values may be sent and summed in bfloat16 or wider, within the bound.
No kernel may reach another device: no remote copies, remote signals or barrier semaphores. Data moves between devices by JAX's collectives and lax.ppermute only.
A program may use at most 64 MiB of HBM per device.

v0:
```python
import jax
import jax.numpy as jnp
from jax import lax
from jax.sharding import Mesh
from jax.sharding import PartitionSpec as P

H = 1024
DP = ("dp_0", "dp_1")
MEMBER = ("member_0", "member_1")
DP_MEMBER = ("dp_0", "dp_1", "member_0", "member_1")


def over_axes(x, axes):
    for axis in axes:
        x = lax.psum(x, axis)
    return x


def sent_together(arrays, axis, dim, along):
    ends, at = ([], 0)
    for a in arrays[:-1]:
        at += a.shape[along]
        ends.append(at)
    both = jnp.concatenate(arrays, axis=along)
    return tuple(jnp.split(lax.all_gather(both, axis, axis=dim, tiled=True), ends, axis=along))


def split_up(x, dim, count):
    lengths = x.shape
    parts = x.reshape(*lengths[:dim], count, lengths[dim] // count, *lengths[dim + 1 :])
    return jnp.moveaxis(parts, dim, 0)


def summed_on_arrival(x, axis, dim):
    count = lax.axis_size(axis)
    parts = lax.all_to_all(split_up(x, dim, count), axis, 0, 0, tiled=True)
    return jnp.sum(parts, axis=0)


def summed_rows(total, axes):
    for axis in axes:
        total = lax.psum_scatter(total, axis, scatter_dimension=0, tiled=True)
    return total


def member_pass(
    picked, goal_rows, lower_weight, lower_shift, upper_weight, upper_shift, log_var, row_count
):
    pre_act = jnp.dot(picked, lower_weight, preferred_element_type=jnp.float32) + lower_shift
    hidden = jax.nn.silu(pre_act).astype(jnp.bfloat16)
    pred_mean = jnp.dot(hidden, upper_weight, preferred_element_type=jnp.float32) + upper_shift
    residual = pred_mean - goal_rows.astype(jnp.float32)
    scaled_err = residual * jnp.exp(-log_var)
    member_loss = 0.5 * jnp.sum(residual * scaled_err + log_var) / row_count
    grad_mean = scaled_err / row_count
    offset_grad = jnp.sum(grad_mean, axis=0)
    noise_grad = 0.5 * jnp.sum(1.0 - residual * scaled_err, axis=0) / row_count
    grad_half = grad_mean.astype(jnp.bfloat16)
    grad_hidden = lax.dot_general(
        grad_half, upper_weight, (((1,), (1,)), ((), ())), preferred_element_type=jnp.float32
    )
    gate_sig = jax.nn.sigmoid(pre_act)
    grad_pre = grad_hidden * gate_sig * (1.0 + pre_act * (1.0 - gate_sig))
    bias_grad = jnp.sum(grad_pre, axis=0)
    pre_half = grad_pre.astype(jnp.bfloat16)
    return (hidden, grad_half, pre_half, bias_grad, offset_grad, noise_grad, member_loss)


def outer_rows(left, right):
    return lax.dot_general(
        left, right, (((0,), (0,)), ((), ())), preferred_element_type=jnp.float32
    )


def feature_stats(inputs):
    values = inputs.astype(jnp.float32)
    row_count = inputs.shape[0] * lax.axis_size(DP) * lax.axis_size(MEMBER)
    col_total, col_squares = (
        over_axes(jnp.sum(values, axis=0), DP_MEMBER),
        over_axes(jnp.sum(values * values, axis=0), DP_MEMBER),
    )
    feature_mean = col_total / row_count
    feature_var = col_squares / row_count - feature_mean * feature_mean
    return (feature_mean, 1.0 / jnp.sqrt(feature_var + 1e-06))


def per_device(
    inputs, targets, bootstrap, lower_weight, lower_shift, upper_weight, upper_shift, log_var
):
    raw_block, goal_block = sent_together((inputs, targets), MEMBER, 0, 1)
    feature_mean, feature_scale = feature_stats(inputs)
    row_block = ((raw_block.astype(jnp.float32) - feature_mean) * feature_scale).astype(
        jnp.bfloat16
    )
    row_count = goal_block.shape[0]
    pick_row = bootstrap[0]
    picked = row_block[pick_row]
    passes = [
        (picked,)
        + member_pass(
            picked,
            goal_block[pick_row],
            lower_weight[0],
            lower_shift[0],
            upper_weight[0],
            upper_shift[0],
            log_var[0],
            row_count,
        )
    ]
    share = H // lax.axis_size(DP)
    lower_list, upper_list = ([], [])
    picked, hidden, grad_half, pre_half, bias_one, offset_one, noise_one, loss_one = passes[0]

    def upper_term(start, count, hidden=hidden, grad_half=grad_half):
        return outer_rows(hidden, grad_half)

    def lower_term(start, count, pre_half=pre_half, picked=picked):
        return outer_rows(pre_half, picked)

    upper_list.append(summed_on_arrival(upper_term(jnp.int32(0), share * lax.axis_size(DP)), DP, 0))
    lower_list.append(summed_rows(lower_term(jnp.int32(0), share * lax.axis_size(DP)), DP))
    lower_grad = jnp.stack(lower_list)
    upper_grad = jnp.stack(upper_list)
    bias_sum = jnp.stack([item[4] for item in passes])
    offset_sum = jnp.stack([item[5] for item in passes])
    noise_sum = jnp.stack([item[6] for item in passes])
    loss_sum = jnp.stack([item[7] for item in passes])
    bias_total, offset_grad, noise_grad, member_loss = (
        over_axes(bias_sum, DP),
        over_axes(offset_sum, DP),
        over_axes(noise_sum, DP),
        over_axes(loss_sum, DP),
    )
    bias_grad = lax.dynamic_slice_in_dim(bias_total, lax.axis_index(DP) * share, share, 1)
    return (lower_grad, bias_grad, upper_grad, offset_grad, noise_grad, member_loss)


def solution(mesh):
    finer = Mesh(mesh.devices.reshape(8, 8, 4, 2), ("dp_0", "dp_1", "member_0", "member_1"))
    return jax.shard_map(
        per_device,
        mesh=finer,
        in_specs=(
            P(DP_MEMBER, None),
            P(DP_MEMBER, None),
            P(MEMBER, DP),
            P(MEMBER, None, None),
            P(MEMBER, None),
            P(MEMBER, None, None),
            P(MEMBER, None),
            P(MEMBER, None),
        ),
        out_specs=(
            P(MEMBER, DP, None),
            P(MEMBER, DP),
            P(MEMBER, DP, None),
            P(MEMBER, None),
            P(MEMBER, None),
            P(MEMBER),
        ),
        check_vma=False,
    )
```

profile of v0, /device:TPU:2, one launch (start us, length us, event | category | flops | bytes accessed | tf_op | source)
XLA Modules:
  0.0 211.3 jit_solution(17410609025989401468)
XLA Ops:
  7.2 0.0 copy-start
  7.2 0.0 all-gather.2.cloned.1.call-start
  7.2 1.9 pad_maximum_fusion
  9.2 0.0 all-gather.2.cloned.1.call-update
  9.2 0.0 reduce-scatter.5.cloned.1.call-start
  9.2 0.7 reduce.1
  9.9 1.0 convert_reduce_fusion
  10.9 23.2 %all-reduce.3 = (f32[393]{0:T(512)S(1)}, f32[393]{0:T(512)S(1)}) all-reduce(f32[393]{0:T(512)S(1)} %get-tuple-element.28, f32[393]{0:T(512)S(1)} %get-tuple-element.27), channel_id=1, replica_groups=mesh['dp_0'=8,'dp_1'=8,'member_0'=4,'member_1'=2] {'dp_0'}, use_global_device_ids=true, to_apply=%region_6.0 | all-reduce | flops 786 | bytes 6288 | tf_op jit(solution)/shard_map/psum | solution.py:15
  34.1 17.6 %all-reduce.1 = (f32[393]{0:T(512)S(1)}, f32[393]{0:T(512)S(1)}) all-reduce(f32[393]{0:T(512)S(1)} %get-tuple-element.41, f32[393]{0:T(512)S(1)} %get-tuple-element.42), channel_id=1, replica_groups=mesh['dp_0'=8,'dp_1'=8,'member_0'=4,'member_1'=2] {'dp_1'}, use_global_device_ids=true, to_apply=%region_7.0 | all-reduce | flops 786 | bytes 6288 | tf_op jit(solution)/shard_map/psum | solution.py:15
  51.7 8.6 %all-reduce.4 = (f32[393]{0:T(512)S(1)}, f32[393]{0:T(512)S(1)}) all-reduce(f32[393]{0:T(512)S(1)} %get-tuple-element.35, f32[393]{0:T(512)S(1)} %get-tuple-element.36), channel_id=1, replica_groups=mesh['dp_0'=8,'dp_1'=8,'member_0'=4,'member_1'=2] {'member_0'}, use_global_device_ids=true, to_apply=%region_8.0 | all-reduce | flops 786 | bytes 6288 | tf_op jit(solution)/shard_map/psum | solution.py:15
  60.3 2.5 %all-reduce.5 = (f32[393]{0:T(512)S(1)}, f32[393]{0:T(512)S(1)}) all-reduce(f32[393]{0:T(512)S(1)} %get-tuple-element.43, f32[393]{0:T(512)S(1)} %get-tuple-element.44), channel_id=1, replica_groups=mesh['dp_0'=8,'dp_1'=8,'member_0'=4,'member_1'=2] {'member_1'}, use_global_device_ids=true, to_apply=%region_9.0 | all-reduce | flops 786 | bytes 6288 | tf_op jit(solution)/shard_map/psum | solution.py:15
  62.8 0.7 fusion.13
  63.5 0.7 fusion.16
  64.2 0.0 all-gather.2.cloned.1.call-done
  64.3 1.8 multiply_convert_fusion.1
  66.1 5.4 %gather_fusion = bf16[1536,393]{1,0:T(8,128)(2,1)} fusion(bf16[1536,393]{1,0:T(8,128)(2,1)S(1)} %multiply_convert_fusion.1, s32[2048]{0:T(1024)S(1)} %pad_clamp_fusion), kind=kCustom, calls=%fused_computation | custom fusion | bytes 2420736 | tf_op jit(solution)/shard_map/gather | solution.py:97
  71.5 1.9 split.9
  73.4 0.0 copy-start.3
  73.4 4.7 %gather_fusion.1 = bf16[1536,377]{1,0:T(8,128)(2,1)S(1)} fusion(bf16[1536,377]{1,0:T(8,128)(2,1)S(1)} %split.9, s32[2048]{0:T(1024)S(1)} %pad_clamp_fusion), kind=kCustom, calls=%fused_computation.1 | custom fusion | bytes 2322432 | tf_op jit(solution)/shard_map/gather | solution.py:102
  78.1 0.0 copy-done
  78.1 0.0 copy-done.3
  78.2 0.0 copy-start.2
  78.2 4.0 %multiply_convert_fusion = (bf16[1536,1024]{1,0:T(8,128)(2,1)S(1)}, f32[1536,1024]{1,0:T(8,128)S(1)}) fusion(f32[1024]{0:T(1024)S(1)} %bitcast.32, bf16[1536,393]{1,0:T(8,128)(2,1)} %gather_fusion, bf16[1,393,1024]{2,1,0:T(8,128)(2,1)S(1)} %copy-done), kind=kOutput, calls=%fused_computation.3 | convolution fusion | flops 1245708288 | bytes 11453440 | tf_op jit(solution)/shard_map/dot_general | solution.py:49
  82.2 0.0 copy-start.4
  82.2 0.0 copy-done.2
  82.2 3.2 %add_reduce_fusion = (f32[]{:T(128)}, f32[377]{0:T(512)S(1)}, f32[377]{0:T(512)S(1)}, f32[1536,377]{1,0:T(8,128)S(1)}) fusion(f32[377]{0:T(512)S(1)} %get-tuple-element.29, f32[377]{0:T(512)S(1)} %get-tuple-element.30, bf16[1536,377]{1,0:T(8,128)(2,1)S(1)} %gather_fusion.1, f32[377]{0:T(512)S(1)} %reduce.1, bf16[1536,1024]{1,0:T(8,128)(2,1)S(1)} %get-tuple-element.49, ...), kind=kOutput, calls=%fused_computation.12 | convolution fusion | flops 1192308480 | bytes 7399800 | tf_op jit(solution)/shard_map/dot_general | solution.py:51
  85.4 0.0 copy-done.4
  85.4 0.0 copy-start.5
  85.4 0.0 copy-start.1
  85.4 3.6 %fusion.17 = (f32[1024]{0:T(1024)S(1)}, bf16[1536,1024]{1,0:T(8,128)(2,1)S(1)}) fusion(f32[1536,1024]{1,0:T(8,128)S(1)} %get-tuple-element.50, f32[1024]{0:T(1024)S(1)} %bitcast.33, bf16[1,1024,377]{2,1,0:T(8,128)(2,1)S(1)} %copy-done.2, f32[1536,377]{1,0:T(8,128)S(1)} %get-tuple-element.53, f32[377]{0:T(512)S(1)} %get-tuple-element.30), kind=kOutput, calls=%fused_computation.36 | convolution fusion | flops 1204977152 | bytes 12535268 | tf_op jit(solution)/shard_map/dot_general | solution.py:59
  89.0 0.0 copy-done.5
  89.0 0.0 copy-done.1
  89.0 2.7 %fusion = f32[1024,393]{0,1:T(8,128)} fusion(bf16[1536,393]{1,0:T(8,128)(2,1)S(1)} %copy-done.1, bf16[1536,1024]{1,0:T(8,128)(2,1)S(1)} %get-tuple-element.52), kind=kOutput, calls=%fused_computation.7 | convolution fusion | flops 1236271104 | bytes 5962752 | tf_op jit(solution)/shard_map/dot_general | solution.py:70
  91.7 0.0 reduce-scatter.5.cloned.1.call-update
  91.8 5.7 %fusion.10 = f32[1024,377]{1,0:T(8,128)} fusion(bf16[1536,1024]{1,0:T(8,128)(2,1)} %copy-done.4, f32[1536,377]{1,0:T(8,128)} %copy-done.5, f32[377]{0:T(512)S(1)} %get-tuple-element.30), kind=kOutput, calls=%fused_computation.24 | convolution fusion | flops 1187676672 | bytes 7007716 | tf_op jit(solution)/shard_map/dot_general | solution.py:70
  97.4 6.2 %all-to-all-start = ((f32[64,16,377]{2,1,0:T(8,128)}), f32[64,16,377]{2,1,0:T(8,128)S(1)}, u32[]{:S(2)}, u32[]{:S(2)}) async-start(f32[64,16,377]{2,1,0:T(8,128)} %bitcast.28), calls=%async_computation.1 | async-start | bytes 3145728 | tf_op jit(solution)/shard_map/all_to_all | solution.py:36
  103.6 0.0 reduce-scatter.7.cloned.1.call-start
  103.7 58.3 %reduce-scatter.5.cloned.1.call-done = f32[128,393]{0,1:T(8,128)} async-done(((f32[1024,393]{0,1:T(8,128)}), f32[128,393]{0,1:T(8,128)}) %reduce-scatter.5.cloned.1.call-update) | async-done | bytes 201232 | tf_op jit(solution)/shard_map/reduce_scatter | solution.py:42
  161.9 1.8 copy.17
  163.7 0.0 reduce-scatter.7.cloned.1.call-update
  164.4 16.8 %all-reduce.2 = (f32[1,1024]{1,0:T(1,128)S(1)}, f32[1,377]{1,0:T(1,128)S(1)}, f32[1,377]{1,0:T(1,128)S(1)}, f32[1]{0:T(128)}) all-reduce(f32[1,1024]{1,0:T(1,128)S(1)} %bitcast.31, f32[1,377]{1,0:T(1,128)S(1)} %stack.19, f32[1,377]{1,0:T(1,128)S(1)} %div.37, ...), channel_id=1, replica_groups=mesh['dp_0'=8,'dp_1'=8,'member_0'=4,'member_1'=2] {'dp_0'}, use_global_device_ids=true, to_apply=%region_13.14 | all-reduce | flops 1779 | bytes 14232 | tf_op jit(solution)/shard_map/psum | solution.py:15
  181.2 18.1 %all-reduce = (f32[1,1024]{1,0:T(1,128)S(1)}, f32[1,377]{1,0:T(1,128)}, f32[1,377]{1,0:T(1,128)}, f32[1]{0:T(128)}) all-reduce(f32[1,1024]{1,0:T(1,128)S(1)} %get-tuple-element.37, f32[1,377]{1,0:T(1,128)S(1)} %get-tuple-element.38, ...), channel_id=1, replica_groups=mesh['dp_0'=8,'dp_1'=8,'member_0'=4,'member_1'=2] {'dp_1'}, use_global_device_ids=true, to_apply=%region_14.15 | all-reduce | flops 1779 | bytes 14232 | tf_op jit(solution)/shard_map/psum | solution.py:15
  199.3 0.6 constant_dynamic-slice_fusion
  199.8 0.0 all-to-all-done
  199.8 0.7 reduce_sum.66
  200.6 2.6 %reduce-scatter.7.cloned.1.call-done = f32[16,393]{1,0:T(8,128)} async-done(((f32[128,393]{1,0:T(8,128)}), f32[16,393]{1,0:T(8,128)}) %reduce-scatter.7.cloned.1.call-update) | async-done | bytes 25168
  203.1 0.9 copy.18
  204.0 0.7 copy.16
  (5 shorter events, 0.0 us)
Async XLA Ops:
  7.2 71.0 %copy-start = (bf16[1,393,1024]{2,1,0:T(8,128)(2,1)S(1)}, bf16[1,393,1024]{2,1,0:T(8,128)(2,1)}, u32[]{:S(2)}) copy-start(bf16[1,393,1024]{2,1,0:T(8,128)(2,1)} %param.11) | copy-start | bytes 2414596
  7.2 57.1 %all-gather.2.cloned.1.call-start = ((), (), s32[]{:S(2)}) async-start(), calls=%async_computation.3 | async-start | bytes 3096576 | tf_op jit(solution)/shard_map/all_gather | solution.py:25
  9.2 152.7 %reduce-scatter.5.cloned.1.call-start = ((), (), s32[]{:S(2)}) async-start(), calls=%async_computation.4 | async-start | bytes 1843200 | tf_op jit(solution)/shard_map/reduce_scatter | solution.py:42
  73.4 4.7 %copy-start.3 = (f32[1,1024]{1,0:T(1,128)S(1)}, f32[1,1024]{1,0:T(1,128)}, u32[]{:S(2)}) copy-start(f32[1,1024]{1,0:T(1,128)} %param.12) | copy-start | bytes 12292
  78.2 4.0 %copy-start.2 = (bf16[1,1024,377]{2,1,0:T(8,128)(2,1)S(1)}, bf16[1,1024,377]{2,1,0:T(8,128)(2,1)}, u32[]{:S(2)}) copy-start(bf16[1,1024,377]{2,1,0:T(8,128)(2,1)} %param.13) | copy-start | bytes 2316292
  82.2 3.2 %copy-start.4 = (bf16[1536,1024]{1,0:T(8,128)(2,1)}, bf16[1536,1024]{1,0:T(8,128)(2,1)S(1)}, u32[]{:S(2)}) copy-start(bf16[1536,1024]{1,0:T(8,128)(2,1)S(1)} %get-tuple-element.49) | copy-start | bytes 9437188
  85.4 3.6 %copy-start.5 = (f32[1536,377]{1,0:T(8,128)}, f32[1536,377]{1,0:T(8,128)S(1)}, u32[]{:S(2)}) copy-start(f32[1536,377]{1,0:T(8,128)S(1)} %get-tuple-element.53) | copy-start | bytes 6948868
  85.4 3.6 %copy-start.1 = (bf16[1536,393]{1,0:T(8,128)(2,1)S(1)}, bf16[1536,393]{1,0:T(8,128)(2,1)}, u32[]{:S(2)}) copy-start(bf16[1536,393]{1,0:T(8,128)(2,1)} %gather_fusion) | copy-start | bytes 3621892
  97.4 102.4 %all-to-all-start = ((f32[64,16,377]{2,1,0:T(8,128)}), f32[64,16,377]{2,1,0:T(8,128)S(1)}, u32[]{:S(2)}, u32[]{:S(2)}) async-start(f32[64,16,377]{2,1,0:T(8,128)} %bitcast.28), calls=%async_computation.1 | async-start | bytes 3145728 | tf_op jit(solution)/shard_map/all_to_all | solution.py:36
  103.6 99.5 %reduce-scatter.7.cloned.1.call-start = ((), (), s32[]{:S(2)}) async-start(), calls=%async_computation.5 | async-start | bytes 294912
Sparse Core Ops, SparseCore 0:
  10.1 35.4 all-gather.1
  91.9 70.0 reduce-scatter.4
  164.7 38.3 reduce-scatter.6
where the time goes:
time: 212 us; the launch traced here: 211 us
  blocking collectives  86.7 us (41%)
  waiting for transfers between devices  60.9 us (29%)
  matrix products  19.2 us (9%)
  local copies, waits for them, and re-layouts  16 us (8%)
  between operations  14.6 us (7%)
  other arithmetic  7.61 us (4%)
  starting transfers between devices  6.32 us (3%)
    psum x6, blocking collectives, over_axes(): x = lax.psum(x, axis)  86.7 us
    reduce_scatter x1, waiting for transfers between devices, summed_rows(): total = lax.psum_scatter(total, axis, scatter_dimension=0, tiled=True)  58.3 us
    dot_general x2, matrix products, outer_rows(): lax.dot_general(left, right, (((0,), (0,)), ((), ())), preferred_element_...  8.34 us
    all_to_all x1, starting transfers between devices, summed_on_arrival(): parts = lax.all_to_all(split_up(x, dim, count), axis, 0, 0, tiled=True)  6.2 us
    gather x1, local copies, waits for them, and re-layouts, per_device(): picked = row_block[pick_row]  5.43 us
    gather x1, local copies, waits for them, and re-layouts, per_device(): goal_block[pick_row]  4.71 us
  transfers between devices with their start and end apart: 4, of which 2 were waited for; matrix products, arithmetic and copies ran while one was open for 6% of the time, Pallas kernels for 0%

commit v1 on v0

--- a/solution.py
+++ b/solution.py
@@ -12,7 +12,8 @@
 
 def over_axes(x, axes):
     for axis in axes:
-        x = lax.psum(x, axis)
+        terms = lax.all_gather(x, axis, axis=0, tiled=False)
+        x = terms.sum(axis=0)
     return x
 
 

time: 212 us -> 332 us (1.57)
  the two profiles are of different devices: /device:TPU:2 before, /device:TPU:4 now
where the time goes in v1:
time: 332 us; the launch traced here: 331 us
  blocking collectives  191 us (58%)
  waiting for transfers between devices  58.3 us (18%)
  local copies, waits for them, and re-layouts  28.3 us (9%)
  matrix products  19.2 us (6%)
  between operations  18.6 us (6%)
  other arithmetic  9.17 us (3%)
  starting transfers between devices  6.53 us (2%)
    unnamed x6, blocking collectives  141 us
    reduce_scatter x1, waiting for transfers between devices, summed_rows(): total = lax.psum_scatter(total, axis, scatter_dimension=0, tiled=True)  58.3 us
    all_gather x2, blocking collectives, over_axes(): terms = lax.all_gather(x, axis, axis=0, tiled=False)  49.3 us
    unnamed x46, local copies, waits for them, and re-layouts  13.6 us
    dot_general x2, matrix products, outer_rows(): lax.dot_general(left, right, (((0,), (0,)), ((), ())), preferred_element_...  8.35 us
  transfers between devices with their start and end apart: 4, of which 1 were waited for; matrix products, arithmetic and copies ran while one was open for 8% of the time, Pallas kernels for 0%

profile of v1, /device:TPU:4, one launch (start us, length us, event | category | flops | bytes accessed | tf_op | source)
XLA Modules:
  0.0 330.9 jit_solution(3211646116791006577)
XLA Ops:
  7.2 1.9 pad_maximum_fusion
  9.2 1.3 dynamic-slice.4
  11.2 1.0 convert_reduce_fusion
  12.2 0.3 dynamic-update-slice
  12.5 0.3 dynamic-update-slice.4
  12.7 35.9 %all-reduce.17 = (f32[3144]{0:T(1024)S(1)}, f32[3144]{0:T(1024)S(1)}) all-reduce(f32[3144]{0:T(1024)S(1)} %dynamic-update-slice.4, f32[3144]{0:T(1024)S(1)} %dynamic-update-slice), channel_id=6, replica_groups=mesh['dp_0'=8,'dp_1'=8,'member_0'=4,'member_1'=2] {'dp_0'}, use_global_device_ids=true, to_apply=%add.4 | all-reduce | flops 6288 | bytes 50304
  48.7 0.1 reshape.94
  48.7 1.3 dynamic-slice.5
  50.7 0.1 reshape.98
  50.8 0.3 dynamic-update-slice.1
  51.1 0.3 dynamic-update-slice.5
  51.3 30.4 %all-reduce.15 = (f32[3144]{0:T(1024)S(1)}, f32[3144]{0:T(1024)S(1)}) all-reduce(f32[3144]{0:T(1024)S(1)} %dynamic-update-slice.5, f32[3144]{0:T(1024)S(1)} %dynamic-update-slice.1), channel_id=7, replica_groups=mesh['dp_0'=8,'dp_1'=8,'member_0'=4,'member_1'=2] {'dp_1'}, use_global_device_ids=true, to_apply=%add.5 | all-reduce | flops 6288 | bytes 50304
  81.7 0.1 reshape.95
  81.8 1.3 dynamic-slice.6
  83.7 0.1 reshape.99
  83.9 0.3 dynamic-update-slice.2
  84.1 0.3 dynamic-update-slice.6
  84.4 14.7 %all-reduce.18 = (f32[1572]{0:T(1024)S(1)}, f32[1572]{0:T(1024)S(1)}) all-reduce(f32[1572]{0:T(1024)S(1)} %dynamic-update-slice.6, f32[1572]{0:T(1024)S(1)} %dynamic-update-slice.2), channel_id=8, replica_groups=mesh['dp_0'=8,'dp_1'=8,'member_0'=4,'member_1'=2] {'member_0'}, use_global_device_ids=true, to_apply=%add.6 | all-reduce | flops 3144 | bytes 25152
  99.1 0.1 reshape.96
  99.2 1.3 dynamic-slice.7
  101.1 0.1 reshape.100
  101.2 0.2 dynamic-update-slice.3
  101.5 0.2 dynamic-update-slice.7
  101.7 2.5 all-reduce.19
  104.1 0.1 reshape.97
  104.2 0.1 reshape.101
  104.3 0.7 reduce.19
  105.0 0.7 fusion.13
  105.8 0.7 fusion.16
  106.5 1.8 multiply_convert_fusion.1
  108.3 5.4 %gather_fusion = bf16[1536,393]{1,0:T(8,128)(2,1)} fusion(bf16[1536,393]{1,0:T(8,128)(2,1)S(1)} %multiply_convert_fusion.1, s32[2048]{0:T(1024)S(1)} %pad_clamp_fusion), kind=kCustom, calls=%fused_computation | custom fusion | bytes 2420736 | tf_op jit(solution)/shard_map/gather | solution.py:98
  113.7 1.9 split.9
  115.7 4.7 %gather_fusion.1 = bf16[1536,377]{1,0:T(8,128)(2,1)S(1)} fusion(bf16[1536,377]{1,0:T(8,128)(2,1)S(1)} %split.9, s32[2048]{0:T(1024)S(1)} %pad_clamp_fusion), kind=kCustom, calls=%fused_computation.1 | custom fusion | bytes 2322432 | tf_op jit(solution)/shard_map/gather | solution.py:103
  120.4 4.0 %multiply_convert_fusion = (bf16[1536,1024]{1,0:T(8,128)(2,1)S(1)}, f32[1536,1024]{1,0:T(8,128)S(1)}) fusion(f32[1024]{0:T(1024)S(1)} %bitcast.42, bf16[1536,393]{1,0:T(8,128)(2,1)} %gather_fusion, bf16[1,393,1024]{2,1,0:T(8,128)(2,1)S(1)} %copy-done), kind=kOutput, calls=%fused_computation.3 | convolution fusion | flops 1245708288 | bytes 11453440 | tf_op jit(solution)/shard_map/dot_general | solution.py:50
  124.4 3.2 add_reduce_fusion
  127.6 3.6 %fusion.17 = (f32[1024]{0:T(1024)S(1)}, bf16[1536,1024]{1,0:T(8,128)(2,1)S(1)}) fusion(f32[1536,1024]{1,0:T(8,128)S(1)} %get-tuple-element.54, f32[1024]{0:T(1024)S(1)} %bitcast.43, bf16[1,1024,377]{2,1,0:T(8,128)(2,1)S(1)} %copy-done.2, f32[1536,377]{1,0:T(8,128)S(1)} %get-tuple-element.57, f32[377]{0:T(512)S(1)} %get-tuple-element.36), kind=kOutput, calls=%fused_computation.36 | convolution fusion | flops 1204977152 | bytes 12535268 | tf_op jit(solution)/shard_map/dot_general | solution.py:60
  131.3 2.7 fusion
  134.0 5.7 %fusion.10 = f32[1024,377]{1,0:T(8,128)} fusion(bf16[1536,1024]{1,0:T(8,128)(2,1)} %copy-done.4, f32[1536,377]{1,0:T(8,128)} %copy-done.5, f32[377]{0:T(512)S(1)} %get-tuple-element.36), kind=kOutput, calls=%fused_computation.24 | convolution fusion | flops 1187676672 | bytes 7007716 | tf_op jit(solution)/shard_map/dot_general | solution.py:71
  139.7 6.4 %all-to-all-start = ((f32[64,16,377]{2,1,0:T(8,128)}), f32[64,16,377]{2,1,0:T(8,128)S(1)}, u32[]{:S(2)}, u32[]{:S(2)}) async-start(f32[64,16,377]{2,1,0:T(8,128)} %bitcast.39), calls=%async_computation.1 | async-start | bytes 3145728 | tf_op jit(solution)/shard_map/all_to_all | solution.py:37
  146.1 0.0 reduce-scatter.7.cloned.1.call-start
  146.1 58.3 %reduce-scatter.5.cloned.1.call-done = f32[128,393]{0,1:T(8,128)} async-done(((f32[1024,393]{0,1:T(8,128)}), f32[128,393]{0,1:T(8,128)}) %reduce-scatter.5.cloned.1.call-update) | async-done | bytes 201232 | tf_op jit(solution)/shard_map/reduce_scatter | solution.py:43
  204.4 1.8 copy.18
  208.1 0.3 dynamic-update-slice.8
  208.4 0.8 dynamic-update-slice.12
  209.2 0.1 multiply_dynamic-update-slice_fusion
  209.3 28.1 %all-reduce.16 = (f32[3016]{0:T(1024)S(1)}, f32[3016]{0:T(1024)S(1)}, f32[8]{0:T(128)S(1)}) all-reduce(f32[3016]{0:T(1024)S(1)} %dynamic-update-slice.8, f32[3016]{0:T(1024)S(1)} %multiply_dynamic-update-slice_fusion, f32[8]{0:T(128)S(1)} %dynamic-update-slice.12), channel_id=12, replica_groups=mesh['dp_0'=8,'dp_1'=8,'member_0'=4,'member_1'=2] {'dp_0'}, use_global_device_ids=true, to_apply=%add.8 | all-reduce | flops 6040 | bytes 48320
  237.4 0.1 reshape.106
  237.5 0.1 reshape.104
  237.6 0.3 dynamic-update-slice.11
  237.9 0.3 dynamic-update-slice.9
  238.1 0.6 reduce.14
  238.7 1.4 dynamic-update-slice.13
  240.2 29.9 %all-reduce.14 = (f32[3016]{0:T(1024)S(1)}, f32[3016]{0:T(1024)S(1)}, f32[8]{0:T(128)S(1)}) all-reduce(f32[3016]{0:T(1024)S(1)} %dynamic-update-slice.9, f32[3016]{0:T(1024)S(1)} %dynamic-update-slice.11, f32[8]{0:T(128)S(1)} %dynamic-update-slice.13), channel_id=13, replica_groups=mesh['dp_0'=8,'dp_1'=8,'member_0'=4,'member_1'=2] {'dp_1'}, use_global_device_ids=true, to_apply=%add.9 | all-reduce | flops 6040 | bytes 48320
  270.0 0.1 reshape.105
  270.2 0.6 reduce_sum.230
  270.7 0.1 reshape.107
  270.8 0.6 reduce_sum.234
  271.4 24.7 %all-gather.8 = f32[8192]{0:T(1024)S(1)} all-gather(f32[1024]{0:T(1024)S(1)} %get-tuple-element.55), channel_id=10, replica_groups=mesh['dp_0'=8,'dp_1'=8,'member_0'=4,'member_1'=2] {'dp_0'}, dimensions={0}, use_global_device_ids=true | all-gather | bytes 36864 | tf_op jit(solution)/shard_map/all_gather | solution.py:15
  296.1 24.7 %all-gather.9 = f32[8192]{0:T(1024)S(1)} all-gather(f32[1024]{0:T(1024)S(1)} %reduce.8), channel_id=11, replica_groups=mesh['dp_0'=8,'dp_1'=8,'member_0'=4,'member_1'=2] {'dp_1'}, dimensions={0}, use_global_device_ids=true | all-gather | bytes 36864 | tf_op jit(solution)/shard_map/all_gather | solution.py:15
  320.8 0.6 reduce.15
  321.4 0.6 dynamic-slice_bitcast_fusion
  322.0 0.7 reduce_sum.226
  322.7 0.9 copy.19
  323.6 0.7 copy.17
  (52 shorter events, 0.5 us)
Async XLA Ops:
  7.2 113.2 %copy-start = (bf16[1,393,1024]{2,1,0:T(8,128)(2,1)S(1)}, bf16[1,393,1024]{2,1,0:T(8,128)(2,1)}, u32[]{:S(2)}) copy-start(bf16[1,393,1024]{2,1,0:T(8,128)(2,1)} %param.11) | copy-start | bytes 2414596
  7.2 99.3 %all-gather.16.cloned.1.call-start = ((), (), s32[]{:S(2)}) async-start(), calls=%async_computation.3 | async-start | bytes 3096576 | tf_op jit(solution)/shard_map/all_gather | solution.py:26
  9.2 195.2 %reduce-scatter.5.cloned.1.call-start = ((), (), s32[]{:S(2)}) async-start(), calls=%async_computation.4 | async-start | bytes 1843200 | tf_op jit(solution)/shard_map/reduce_scatter | solution.py:43
  115.7 4.7 %copy-start.3 = (f32[1,1024]{1,0:T(1,128)S(1)}, f32[1,1024]{1,0:T(1,128)}, u32[]{:S(2)}) copy-start(f32[1,1024]{1,0:T(1,128)} %param.12) | copy-start | bytes 12292
  120.4 4.0 %copy-start.2 = (bf16[1,1024,377]{2,1,0:T(8,128)(2,1)S(1)}, bf16[1,1024,377]{2,1,0:T(8,128)(2,1)}, u32[]{:S(2)}) copy-start(bf16[1,1024,377]{2,1,0:T(8,128)(2,1)} %param.13) | copy-start | bytes 2316292
  124.4 3.2 copy-start.4
  127.6 3.6 %copy-start.5 = (f32[1536,377]{1,0:T(8,128)}, f32[1536,377]{1,0:T(8,128)S(1)}, u32[]{:S(2)}) copy-start(f32[1536,377]{1,0:T(8,128)S(1)} %get-tuple-element.57) | copy-start | bytes 6948868
  127.6 3.6 %copy-start.1 = (bf16[1536,393]{1,0:T(8,128)(2,1)S(1)}, bf16[1536,393]{1,0:T(8,128)(2,1)}, u32[]{:S(2)}) copy-start(bf16[1536,393]{1,0:T(8,128)(2,1)} %gather_fusion) | copy-start | bytes 3621892
  139.7 182.3 %all-to-all-start = ((f32[64,16,377]{2,1,0:T(8,128)}), f32[64,16,377]{2,1,0:T(8,128)S(1)}, u32[]{:S(2)}, u32[]{:S(2)}) async-start(f32[64,16,377]{2,1,0:T(8,128)} %bitcast.39), calls=%async_computation.1 | async-start | bytes 3145728 | tf_op jit(solution)/shard_map/all_to_all | solution.py:37
  146.1 176.6 %reduce-scatter.7.cloned.1.call-start = ((), (), s32[]{:S(2)}) async-start(), calls=%async_computation.5 | async-start | bytes 294912
Sparse Core Ops, SparseCore 0:
  10.1 35.3 all-gather.15
  134.1 70.2 reduce-scatter.4
  207.2 38.3 reduce-scatter.6
